TPU v7x, 256 devices: a 4x2x16 block of a 4x16x16 slice. The times are simulated.
256 devices in a mesh: chain: 2 (over y), gz: 16 (over z), gy: 4 (over x), pa: 2 (over core).
Axes of the slice: x: 4, y: 2, z: 16, core: 2. Of those that a mesh axis runs over, the one named last changes fastest.
The devices are a block of a 4x16x16 slice.
Arguments:
- probes: float32 [32, 128, 128, 256], P(('chain', 'pa'), 'gz', 'gy'), parts along dimension 0, may hold values from -6 to 6
- velocity: float32 [3, 256, 128, 256], P(None, ('chain', 'gz'), 'gy'), parts along dimension 1, may hold values from -0.3 to 0.3
- prior_scale: float32 [256, 128, 256], P(('chain', 'gz'), 'gy'), parts along dimension 0, may hold values from 0.3 to 3
- noise_precision: float32 [256, 128, 256], P(('chain', 'gz'), 'gy'), parts along dimension 0, may hold values from 0.3 to 3
- source_mask: int32 [256, 128, 256], P(('chain', 'gz'), 'gy'), parts along dimension 0, may hold values 0 or 1
- sensor_mask: int32 [256, 128, 256], P(('chain', 'gz'), 'gy'), parts along dimension 0, may hold values 0 or 1
Outputs:
- hessian: float32 [32, 128, 128, 256], P(('chain', 'pa'), 'gz', 'gy'), parts along dimension 0
- gram: float32 [32, 16], P(('chain', 'pa')), parts along dimension 0
There are 2 independent parts, one for each index of `chain`. A program takes and returns all parts, laid end to end along the dimension named above; each array names one. Nothing has to cross between parts.
All inputs are finite; a program needn't handle non-finite values. No bound on the sum of `source_mask` or of `sensor_mask` on one device may be relied on, other than what follows from the above.
Results may differ from a plain program's by a relative error of at most 0.0003.
Values sent between devices are 32-bit elements; how exact they have to be, the bound alone decides.
A program may use at most 128 MiB of HBM per device.

v0:
```python
import functools

import jax
import jax.numpy as jnp
import numpy as np
from jax import lax
from jax.experimental import pallas as pl
from jax.experimental.pallas import tpu as pltpu
from jax.sharding import PartitionSpec as P

MESH = pl.DeviceIdType.MESH
STEPS = 5
SUB = 8

diffuse_cross = 0.15
diffuse_along = 16.0

ZLO, ZHI, YLO, YHI = range(4)
CZP, CZM, CYP, CYM, CXP, CXM, SRC, OBS = range(8)


def implicit_matrix(length):
    banded = (1.0 + 2.0 * diffuse_along) * np.eye(length) - diffuse_along * (
        np.eye(length, k=1) + np.eye(length, k=-1)
    )
    matrix = np.linalg.inv(banded).astype(np.float32)
    high = matrix.astype(jnp.bfloat16)
    low = (matrix - high.astype(np.float32)).astype(jnp.bfloat16)
    return jnp.asarray(high), jnp.asarray(low)


def kernel(
    probes_ref,
    vel_ref,
    prior_ref,
    noise_ref,
    smask_ref,
    omask_ref,
    mhi_ref,
    mlo_ref,
    out_ref,
    u_ref,
    s_ref,
    b_ref,
    coef_ref,
    whi_ref,
    wlo_ref,
    zh_ref,
    yh_ref,
    zs_ref,
    ys_ref,
    send_sem,
    recv_sem,
):
    count, nz, ny, nx = probes_ref.shape
    tiles = ny // SUB
    zi, yi = lax.axis_index("gz"), lax.axis_index("gy")
    zn, yn = lax.axis_size("gz"), lax.axis_size("gy")
    exists = [zi > 0, zi < zn - 1, yi > 0, yi < yn - 1]
    target = [
        {"gz": lax.max(zi - 1, 0)},
        {"gz": lax.min(zi + 1, zn - 1)},
        {"gy": lax.max(yi - 1, 0)},
        {"gy": lax.min(yi + 1, yn - 1)},
    ]

    barrier = pltpu.get_barrier_semaphore()
    for side in range(4):

        @pl.when(exists[side])
        def _():
            pl.semaphore_signal(barrier, inc=1, device_id=target[side], device_id_type=MESH)

    row = lax.broadcasted_iota(jnp.int32, (SUB, nx), 0)
    first_row, last_row = row == 0, row == SUB - 1
    lane = lax.broadcasted_iota(jnp.int32, (ny, nx), 1)

    def prepare(z, _):
        vx, vy, vz = (0.5 * vel_ref[c, z] for c in range(3))
        coef_ref[CZP, z] = diffuse_cross - vz
        coef_ref[CZM, z] = diffuse_cross + vz
        coef_ref[CYP, z] = diffuse_cross - vy
        coef_ref[CYM, z] = diffuse_cross + vy
        coef_ref[CXP, z] = jnp.where(lane == nx - 1, 0.0, -vx)
        coef_ref[CXM, z] = jnp.where(lane == 0, 0.0, vx)
        coef_ref[SRC, z] = smask_ref[z].astype(jnp.float32) * prior_ref[z]
        coef_ref[OBS, z] = omask_ref[z].astype(jnp.float32) * noise_ref[z]
        return 0

    lax.fori_loop(0, nz, prepare, 0)

    @pl.when(zi == 0)
    def _():
        zh_ref[:, 0] = jnp.zeros(zh_ref.shape[:1] + zh_ref.shape[2:], jnp.float32)

    @pl.when(zi == zn - 1)
    def _():
        zh_ref[:, 1] = jnp.zeros(zh_ref.shape[:1] + zh_ref.shape[2:], jnp.float32)

    @pl.when(yi == 0)
    def _():
        yh_ref[:, 0] = jnp.zeros(yh_ref.shape[:1] + yh_ref.shape[2:], jnp.float32)

    @pl.when(yi == yn - 1)
    def _():
        yh_ref[:, 1] = jnp.zeros(yh_ref.shape[:1] + yh_ref.shape[2:], jnp.float32)

    pl.semaphore_wait(barrier, sum(side.astype(jnp.int32) for side in exists))

    def copies(slot, p, sources):
        result = []
        for side in range(4):
            halo = zh_ref if side < 2 else yh_ref
            result.append(
                pltpu.make_async_remote_copy(
                    src_ref=sources[side],
                    dst_ref=halo.at[slot, (side % 2) ^ 1, p],
                    send_sem=send_sem.at[slot, side, p],
                    recv_sem=recv_sem.at[slot, side ^ 1, p],
                    device_id=target[side],
                    device_id_type=MESH,
                )
            )
        return result

    def send(slot, p, sources):
        for side, copy in enumerate(copies(slot, p, sources)):
            pl.when(exists[side])(copy.start)

    def settle(slot, p, sources):
        moved = copies(slot, p, sources)
        for side in range(4):

            @pl.when(exists[side])
            def _():
                moved[side ^ 1].wait_recv()
                moved[side].wait_send()

    def state_sources(n, slot, p):
        return [u_ref.at[n, p, 0], u_ref.at[n, p, nz - 1], ys_ref.at[slot, 0, p], ys_ref.at[slot, 1, p]]

    def adjoint_sources(slot, p):
        return [zs_ref.at[slot, 0, p], zs_ref.at[slot, 1, p], ys_ref.at[slot, 0, p], ys_ref.at[slot, 1, p]]

    def put(z, pair, left, right):
        rows = jnp.concatenate([left, right], axis=0)
        high = rows.astype(jnp.bfloat16)
        low = (rows - high.astype(jnp.float32)).astype(jnp.bfloat16)
        where = pl.ds(z * ny + pair * 2 * SUB, 2 * SUB)
        whi_ref[where, :] = high
        wlo_ref[where, :] = low

    def solve():
        dot = functools.partial(jnp.dot, preferred_element_type=jnp.float32)
        high, low = whi_ref[...], wlo_ref[...]
        moved = dot(high, mhi_ref[...]) + (dot(high, mlo_ref[...]) + dot(low, mhi_ref[...]))
        return moved.reshape(nz, ny, nx)

    def by_tile(make):
        for z in range(nz):
            for pair in range(tiles // 2):
                put(z, pair, make(z, 2 * pair), make(z, 2 * pair + 1))

    def rows_of(t):
        return pl.ds(t * SUB, SUB)

    def coef(kind, z, t):
        return coef_ref[kind, z, rows_of(t), :]

    def forward(n, slot, p):
        def make(z, t):
            def at(zz, tt):
                return u_ref[n, p, zz, rows_of(tt), :]

            centre = at(z, t)
            plus_z = at(z + 1, t) if z < nz - 1 else zh_ref[slot, 1, p, rows_of(t), :]
            minus_z = at(z - 1, t) if z > 0 else zh_ref[slot, 0, p, rows_of(t), :]
            if t < tiles - 1:
                above = pltpu.roll(at(z, t + 1), SUB - 1, 0)
            else:
                above = jnp.broadcast_to(yh_ref[slot, 1, p, pl.ds(z, 1), :], (SUB, nx))
            if t > 0:
                below = pltpu.roll(at(z, t - 1), 1, 0)
            else:
                below = jnp.broadcast_to(yh_ref[slot, 0, p, pl.ds(z, 1), :], (SUB, nx))
            plus_y = jnp.where(last_row, above, pltpu.roll(centre, SUB - 1, 0))
            minus_y = jnp.where(first_row, below, pltpu.roll(centre, 1, 0))
            total = (1.0 - 4.0 * diffuse_cross) * centre + s_ref[p, z, rows_of(t), :]
            total = total + (coef(CZP, z, t) * plus_z + coef(CZM, z, t) * minus_z)
            total = total + (coef(CYP, z, t) * plus_y + coef(CYM, z, t) * minus_y)
            return total + (
                coef(CXP, z, t) * pltpu.roll(centre, nx - 1, 1) + coef(CXM, z, t) * pltpu.roll(centre, 1, 1)
            )

        by_tile(make)

    def backward(n, slot, p):
        def make(z, t):
            def at(zz, tt):
                return b_ref[p, zz, rows_of(tt), :]

            centre = at(z, t)
            if z < nz - 1:
                plus_z = coef(CZM, z + 1, t) * at(z + 1, t)
            else:
                plus_z = zh_ref[slot, 1, p, rows_of(t), :]
            if z > 0:
                minus_z = coef(CZP, z - 1, t) * at(z - 1, t)
            else:
                minus_z = zh_ref[slot, 0, p, rows_of(t), :]
            if t < tiles - 1:
                above = pltpu.roll(coef(CYM, z, t + 1) * at(z, t + 1), SUB - 1, 0)
            else:
                above = jnp.broadcast_to(yh_ref[slot, 1, p, pl.ds(z, 1), :], (SUB, nx))
            if t > 0:
                below = pltpu.roll(coef(CYP, z, t - 1) * at(z, t - 1), 1, 0)
            else:
                below = jnp.broadcast_to(yh_ref[slot, 0, p, pl.ds(z, 1), :], (SUB, nx))
            plus_y = jnp.where(last_row, above, pltpu.roll(coef(CYM, z, t) * centre, SUB - 1, 0))
            minus_y = jnp.where(first_row, below, pltpu.roll(coef(CYP, z, t) * centre, 1, 0))
            total = (1.0 - 4.0 * diffuse_cross) * centre + coef(OBS, z, t) * u_ref[n, p, z, rows_of(t), :]
            total = total + (plus_z + minus_z)
            total = total + (plus_y + minus_y)
            return total + (
                pltpu.roll(coef(CXM, z, t) * centre, nx - 1, 1) + pltpu.roll(coef(CXP, z, t) * centre, 1, 1)
            )

        by_tile(make)

    def finish_state(n, slot, p):
        state = solve()
        u_ref[n, p] = state
        for z in range(nz):
            ys_ref[slot, 0, p, pl.ds(z, 1), :] = state[z, 0:1, :]
            ys_ref[slot, 1, p, pl.ds(z, 1), :] = state[z, ny - 1 : ny, :]

    def finish_adjoint(slot, p, pulled):
        b_ref[p] = pulled
        zs_ref[slot, 0, p] = coef_ref[CZM, 0] * pulled[0]
        zs_ref[slot, 1, p] = coef_ref[CZP, nz - 1] * pulled[nz - 1]
        for z in range(nz):
            ys_ref[slot, 0, p, pl.ds(z, 1), :] = coef_ref[CYM, z, 0:1, :] * pulled[z, 0:1, :]
            ys_ref[slot, 1, p, pl.ds(z, 1), :] = coef_ref[CYP, z, ny - 1 : ny, :] * pulled[z, ny - 1 : ny, :]

    last = STEPS - 1

    def first_step(p, _):
        for z in range(nz):
            for t in range(tiles):
                s_ref[p, z, rows_of(t), :] = coef(SRC, z, t) * probes_ref[p, z, rows_of(t), :]
        by_tile(lambda z, t: coef(SRC, z, t) * probes_ref[p, z, rows_of(t), :])
        finish_state(0, 0, p)
        send(0, p, state_sources(0, 0, p))
        return 0

    lax.fori_loop(0, count, first_step, 0)

    def forward_step(i, _):
        n, p = i // count + 1, i % count
        before, now = (n + 1) % 2, n % 2
        settle(before, p, state_sources(n - 1, before, p))
        forward(n - 1, before, p)
        finish_state(n, now, p)
        send(now, p, state_sources(n, now, p))
        return 0

    lax.fori_loop(0, (last - 1) * count, forward_step, 0)

    def turn_step(p, _):
        before, now = (last + 1) % 2, last % 2
        settle(before, p, state_sources(last - 1, before, p))
        forward(last - 1, before, p)
        u_ref[last, p] = solve()
        by_tile(lambda z, t: coef(OBS, z, t) * u_ref[last, p, z, rows_of(t), :])
        pulled = solve()
        out_ref[p] = pulled
        finish_adjoint(now, p, pulled)
        send(now, p, adjoint_sources(now, p))
        return 0

    lax.fori_loop(0, count, turn_step, 0)

    def backward_step(i, _):
        k, p = i // count + 1, i % count
        before, now = (last + k + 1) % 2, (last + k) % 2
        settle(before, p, adjoint_sources(before, p))
        backward(last - k, before, p)
        pulled = solve()
        out_ref[p] += pulled
        finish_adjoint(now, p, pulled)
        send(now, p, adjoint_sources(now, p))
        return 0

    lax.fori_loop(0, (last - 1) * count, backward_step, 0)

    def last_step(p, _):
        before = (2 * last + 1) % 2
        settle(before, p, adjoint_sources(before, p))
        backward(0, before, p)
        out_ref[p] = coef_ref[SRC] * (out_ref[p] + solve())
        return 0

    lax.fori_loop(0, count, last_step, 0)


def by_axis(array, axes):
    return functools.reduce(lax.psum, axes, array)


def shards(probes, velocity, prior_scale, noise_precision, source_mask, sensor_mask):
    count, nz, ny, nx = probes.shape
    high, low = implicit_matrix(nx)
    vmem = pl.BlockSpec(memory_space=pltpu.VMEM)
    hessian = pl.pallas_call(
        kernel,
        out_shape=jax.ShapeDtypeStruct(probes.shape, jnp.float32),
        in_specs=[vmem] * 8,
        out_specs=vmem,
        scratch_shapes=[
            pltpu.VMEM((STEPS, count, nz, ny, nx), jnp.float32),
            pltpu.VMEM((count, nz, ny, nx), jnp.float32),
            pltpu.VMEM((count, nz, ny, nx), jnp.float32),
            pltpu.VMEM((8, nz, ny, nx), jnp.float32),
            pltpu.VMEM((nz * ny, nx), jnp.bfloat16),
            pltpu.VMEM((nz * ny, nx), jnp.bfloat16),
            pltpu.VMEM((2, 2, count, ny, nx), jnp.float32),
            pltpu.VMEM((2, 2, count, nz, nx), jnp.float32),
            pltpu.VMEM((2, 2, count, ny, nx), jnp.float32),
            pltpu.VMEM((2, 2, count, nz, nx), jnp.float32),
            pltpu.SemaphoreType.DMA((2, 4, count)),
            pltpu.SemaphoreType.DMA((2, 4, count)),
        ],
        compiler_params=pltpu.CompilerParams(
            collective_id=0, has_side_effects=True, vmem_limit_bytes=48 * 1024 * 1024
        ),
        name="solve",
    )(probes, velocity, prior_scale, noise_precision, source_mask, sensor_mask, high, low)
    own_rows = probes.reshape(count, -1)
    piece = lax.all_gather(hessian, "pa", axis=0, tiled=True)
    partial_gram = jnp.einsum(
        "ac,bc->ab", own_rows, piece.reshape(piece.shape[0], -1), precision=lax.Precision.HIGHEST
    )
    total_cells = nz * ny * nx * lax.axis_size("gz") * lax.axis_size("gy")
    gram = by_axis(partial_gram, ("gz", "gy")) / total_cells
    return (hessian, gram)


def solution(mesh):
    in_specs = (
        P(("chain", "pa"), "gz", "gy", None),
        P(None, ("chain", "gz"), "gy", None),
        P(("chain", "gz"), "gy", None),
        P(("chain", "gz"), "gy", None),
        P(("chain", "gz"), "gy", None),
        P(("chain", "gz"), "gy", None),
    )
    out_specs = (P(("chain", "pa"), "gz", "gy", None), P(("chain", "pa"), None))
    return jax.shard_map(shards, mesh=mesh, in_specs=in_specs, out_specs=out_specs, check_vma=False)
```

profile of v0, /device:TPU:40, one launch (start us, length us, event | category | flops | bytes accessed | tf_op | source)
XLA Modules:
  0.0 165.3 jit_solution(2067665517289713645)
XLA Ops:
  7.2 0.1 all-gather.2.cloned.1.call-start
  7.2 0.0 copy-start
  7.3 1.1 copy-done
  8.4 0.0 copy-start.1
  8.4 0.9 copy-done.1
  9.3 0.0 copy-start.2
  9.3 0.9 copy-done.2
  10.3 0.0 copy-start.3
  10.3 0.9 copy-done.3
  11.2 0.0 copy-start.4
  11.2 0.9 copy-done.4
  12.2 0.0 copy-start.5
  12.2 0.9 copy-done.5
  13.1 0.9 copy-done.6
  14.0 58.9 %solve.1 = f32[8,8,32,256]{3,2,1,0:T(8,128)} custom-call(f32[8,8,32,256]{3,2,1,0:T(8,128)} %probes_ref.1, f32[3,8,32,256]{3,2,1,0:T(8,128)S(1)} %copy-done, f32[8,32,256]{2,1,0:T(8,128)S(1)} %copy-done.1, f32[8,32,256]{2,1,0:T(8,128)S(1)} %copy-done.2, s32[8,32,256]{2,1,0:T(8,128)S(1)} %copy-done.3, s32[8,32,256]{2,1,0:T(8,128)S(1)} %copy-done.4, ...), custom_call_target="tpu_custom_call" | custom-call | tf_op jit(solution)/shard_map/solve/pallas_call | solution.py:314
  73.0 0.0 copy-start.7
  73.0 0.1 all-gather.2.cloned.1.call-update
  73.0 30.9 %all-gather.2.cloned.1.call-done = f32[16,8,32,256]{3,2,1,0:T(8,128)} async-done(((f32[8,8,32,256]{3,2,1,0:T(8,128)}), f32[16,8,32,256]{3,2,1,0:T(8,128)}) %all-gather.2.cloned.1.call-update) | async-done | bytes 4194320 | tf_op jit(solution)/shard_map/all_gather | solution.py:339
  103.9 0.0 copy-done.7
  103.9 9.2 %fusion.3 = f32[8,16]{1,0:T(8,128)S(1)} fusion(f32[8,8,32,256]{3,2,1,0:T(8,128)S(1)} %copy-done.7, f32[16,8,32,256]{3,2,1,0:T(8,128)} %all-gather.2.cloned.1.call-done), kind=kOutput, calls=%fused_computation.3 | convolution fusion | flops 100663296 | bytes 6291968 | tf_op jit(solution)/shard_map/ac,bc->ab/dot_general | solution.py:340
  113.1 31.1 %psum.14 = f32[8,16]{1,0:T(8,128)S(1)} all-reduce(f32[8,16]{1,0:T(8,128)S(1)} %fusion.3), channel_id=1, replica_groups=mesh['chain'=2,'gz'=16,'gy'=4,'pa'=2] {'gz'}, use_global_device_ids=true, to_apply=%region_0.0 | all-reduce | flops 128 | bytes 1024 | tf_op jit(solution)/shard_map/psum | solution.py:307
  144.2 10.5 %psum.15 = f32[8,16]{1,0:T(8,128)S(1)} all-reduce(f32[8,16]{1,0:T(8,128)S(1)} %psum.14), channel_id=1, replica_groups=mesh['chain'=2,'gz'=16,'gy'=4,'pa'=2] {'gy'}, use_global_device_ids=true, to_apply=%region_1.0 | all-reduce | flops 128 | bytes 1024 | tf_op jit(solution)/shard_map/psum | solution.py:307
  154.7 0.6 broadcast_multiply_fusion
  155.3 3.2 %copy.24 = f32[8,8,32,256]{3,2,1,0:T(8,128)} copy(f32[8,8,32,256]{3,2,1,0:T(8,128)} %solve.1) | data formatting | bytes 4194304
  (1 shorter events, 0.0 us)
Async XLA Ops:
  7.2 96.7 %all-gather.2.cloned.1.call-start = ((), (), s32[]{:S(2)}) async-start(), calls=%async_computation | async-start | bytes 6291456 | tf_op jit(solution)/shard_map/all_gather | solution.py:339
  7.2 1.1 copy-start
  8.4 0.9 copy-start.1
  9.3 0.9 copy-start.2
  10.3 0.9 copy-start.3
  11.2 0.9 copy-start.4
  12.2 0.9 copy-start.5
  13.1 0.9 copy-start.6
  73.0 31.0 %copy-start.7 = (f32[8,8,32,256]{3,2,1,0:T(8,128)S(1)}, f32[8,8,32,256]{3,2,1,0:T(8,128)}, u32[]{:S(2)}) copy-start(f32[8,8,32,256]{3,2,1,0:T(8,128)} %probes_ref.1) | copy-start | bytes 6291460
Sparse Core Ops, SparseCore 0:
  73.1 30.7 all-gather.1
where the time goes:
time: 166 us; the launch traced here: 165 us
  Pallas kernels  58.9 us (35%)
  blocking collectives  41.6 us (25%)
  waiting for transfers between devices  31 us (19%)
  between operations  14.1 us (8%)
  local copies, waits for them, and re-layouts  9.9 us (6%)
  matrix products  9.18 us (6%)
    pallas_call x1, Pallas kernels, shards(): pl.pallas_call(kernel, out_shape=jax.ShapeDtypeStruct(probes.shape, jnp.f...  58.9 us
    psum x2, blocking collectives, by_axis(): return functools.reduce(lax.psum, axes, array)  41.6 us
    all_gather x1, waiting for transfers between devices, shards(): piece = lax.all_gather(hessian, 'pa', axis=0, tiled=True)  30.9 us
    unnamed x17, local copies, waits for them, and re-layouts  9.9 us
    dot_general x1, matrix products, shards(): jnp.einsum('ac,bc->ab', own_rows, piece.reshape(piece.shape[0], -1), prec...  9.18 us
  transfers between devices with their start and end apart: 1, of which 1 were waited for; matrix products, arithmetic and copies ran while one was open for 0% of the time, Pallas kernels for 0%

commit v1 on v0

--- a/solution.py
+++ b/solution.py
@@ -30,15 +30,12 @@
 
 
 def kernel(
-    probes_ref,
-    vel_ref,
-    prior_ref,
-    noise_ref,
-    smask_ref,
-    omask_ref,
-    mhi_ref,
-    mlo_ref,
-    out_ref,
+    *refs,
+):
+    inputs, (hessian_ref, gram_ref), refs = refs[:8], refs[8:10], refs[10:]
+    loaded, refs = refs[:8], refs[8:]
+    probes_ref, vel_ref, prior_ref, noise_ref, smask_ref, omask_ref, mhi_ref, mlo_ref = loaded
+    (
     u_ref,
     s_ref,
     b_ref,
@@ -51,7 +48,19 @@
     ys_ref,
     send_sem,
     recv_sem,
-):
+    load_sem,
+    out_ref,
+    out_sem,
+    pu_ref,
+    acc_ref,
+    sum_ref,
+    gt_ref,
+    gr_ref,
+    pair_send,
+    pair_recv,
+    tile_send,
+    tile_recv,
+    ) = refs
     count, nz, ny, nx = probes_ref.shape
     tiles = ny // SUB
     zi, yi = lax.axis_index("gz"), lax.axis_index("gy")
@@ -64,12 +73,44 @@
         {"gy": lax.min(yi + 1, yn - 1)},
     ]
 
+    own = lax.axis_index("pa")
+    half = nz // 2
+
+    def crossed(me, distance):
+        return me + distance * (1 - 2 * ((me // distance) % 2))
+
+    rounds = [{"pa": 1 - own}]
+    for axis, me, n in (("gy", yi, yn), ("gz", zi, zn)):
+        distance = 1
+        while distance < n:
+            rounds.append({axis: crossed(me, distance)})
+            distance *= 2
+    far = 1 if zn > 8 else 0
+    z_other = zi - 1 + 2 * (zi % 2)
+    y_other = yi - 1 + 2 * (yi % 2)
+    met = [
+        ((z_other >= 0) & (z_other < zn), {"gz": lax.clamp(0, z_other, zn - 1)}),
+        ((y_other >= 0) & (y_other < yn), {"gy": lax.clamp(0, y_other, yn - 1)}),
+    ]
+
+    probe_loads = [
+        pltpu.make_async_copy(inputs[0].at[p], probes_ref.at[p], load_sem.at[8 + p]) for p in range(count)
+    ]
+    loads = [None] + [pltpu.make_async_copy(inputs[k], loaded[k], load_sem.at[k]) for k in range(1, 8)]
+    for copy in (loads[2], loads[4], probe_loads[0], loads[6], loads[7], *probe_loads[1:]):
+        copy.start()
+    for copy in (loads[1], loads[3], loads[5]):
+        copy.start()
+
     barrier = pltpu.get_barrier_semaphore()
-    for side in range(4):
-
-        @pl.when(exists[side])
-        def _():
-            pl.semaphore_signal(barrier, inc=1, device_id=target[side], device_id_type=MESH)
+    greeted = rounds[: len(rounds) - far]
+    for device in greeted:
+        pl.semaphore_signal(barrier, inc=1, device_id=device, device_id_type=MESH)
+    for there, device in met:
+
+        @pl.when(there)
+        def _():
+            pl.semaphore_signal(barrier, inc=1, device_id=device, device_id_type=MESH)
 
     row = lax.broadcasted_iota(jnp.int32, (SUB, nx), 0)
     first_row, last_row = row == 0, row == SUB - 1
@@ -83,11 +124,8 @@
         coef_ref[CYM, z] = diffuse_cross + vy
         coef_ref[CXP, z] = jnp.where(lane == nx - 1, 0.0, -vx)
         coef_ref[CXM, z] = jnp.where(lane == 0, 0.0, vx)
-        coef_ref[SRC, z] = smask_ref[z].astype(jnp.float32) * prior_ref[z]
         coef_ref[OBS, z] = omask_ref[z].astype(jnp.float32) * noise_ref[z]
         return 0
-
-    lax.fori_loop(0, nz, prepare, 0)
 
     @pl.when(zi == 0)
     def _():
@@ -105,7 +143,13 @@
     def _():
         yh_ref[:, 1] = jnp.zeros(yh_ref.shape[:1] + yh_ref.shape[2:], jnp.float32)
 
-    pl.semaphore_wait(barrier, sum(side.astype(jnp.int32) for side in exists))
+    acc_ref[...] = jnp.zeros(acc_ref.shape, jnp.float32)
+    loads[2].wait()
+    loads[4].wait()
+    coef_ref[SRC] = smask_ref[...].astype(jnp.float32) * prior_ref[...]
+    loads[6].wait()
+    loads[7].wait()
+    pl.semaphore_wait(barrier, len(greeted) + sum(there.astype(jnp.int32) for there, _ in met))
 
     def copies(slot, p, sources):
         result = []
@@ -242,9 +286,124 @@
             ys_ref[slot, 0, p, pl.ds(z, 1), :] = coef_ref[CYM, z, 0:1, :] * pulled[z, 0:1, :]
             ys_ref[slot, 1, p, pl.ds(z, 1), :] = coef_ref[CYP, z, ny - 1 : ny, :] * pulled[z, ny - 1 : ny, :]
 
+    def pair_copy(n):
+        return pltpu.make_async_remote_copy(
+            src_ref=u_ref.at[n, :, pl.ds((1 - own) * half, half)],
+            dst_ref=pu_ref.at[n],
+            send_sem=pair_send.at[n],
+            recv_sem=pair_recv.at[n],
+            device_id=rounds[0],
+            device_id_type=MESH,
+        )
+
+    def tile_copy(k):
+        return pltpu.make_async_remote_copy(
+            src_ref=gt_ref.at[k if k == 0 else k + 1],
+            dst_ref=gr_ref.at[k],
+            send_sem=tile_send.at[k],
+            recv_sem=tile_recv.at[k],
+            device_id=rounds[k],
+            device_id_type=MESH,
+        )
+
+    near = count // 2 + 1
+    lanes = 128
+    pieces = [(t, h) for t in range(tiles) for h in range(nx // lanes)]
+
+    def gram_unit(n, i):
+        if count != 8:
+            raise NotImplementedError
+        wait_pair = pl.when(i == 0)
+
+        @wait_pair
+        def _():
+            pair_copy(n).wait()
+
+        def own_terms(z, sums):
+            sums = list(sums)
+            for t, h in pieces:
+                where = (rows_of(t), pl.ds(h * lanes, lanes))
+                x = [u_ref[(n, (i + d) % count, z) + where] for d in range(near + 1)]
+                weight = coef_ref[(OBS, z) + where]
+                for r in range(2):
+                    scaled = weight * x[r]
+                    for d in range(near):
+                        sums[r * near + d] = sums[r * near + d] + scaled * x[r + d]
+            return tuple(sums)
+
+        def pair_terms(z, sums):
+            sums = list(sums)
+            for t, h in pieces:
+                where = (rows_of(t), pl.ds(h * lanes, lanes))
+                weight = coef_ref[(OBS, own * half + z) + where]
+                scaled = [weight * u_ref[(n, i + r, own * half + z) + where] for r in range(2)]
+                for j in range(count):
+                    y = pu_ref[(n, j, z) + where]
+                    for r in range(2):
+                        sums[r * count + j] = sums[r * count + j] + scaled[r] * y
+            return tuple(sums)
+
+        zero = jnp.zeros((SUB, lanes), jnp.float32)
+        sums = lax.fori_loop(0, nz, own_terms, (zero,) * (2 * near))
+        for r in range(2):
+            for d in range(near):
+                acc_ref[i + r, d] += sums[r * near + d]
+        sums = lax.fori_loop(0, half, pair_terms, (zero,) * (2 * count))
+        for r in range(2):
+            for j in range(count):
+                acc_ref[i + r, near + j] += sums[r * count + j]
+
+    def gram_tile():
+        ones = jnp.ones((lanes, lanes), jnp.float32)
+        kinds = near + count
+
+        def by_lanes(i, _):
+            partial = acc_ref[i].reshape(kinds * SUB, lanes)
+            total = jnp.dot(
+                partial, ones, precision=lax.Precision.HIGHEST, preferred_element_type=jnp.float32
+            )
+            sum_ref[i] = total.reshape(kinds, SUB, lanes)
+            return 0
+
+        lax.fori_loop(0, count, by_lanes, 0)
+        at_row = lax.broadcasted_iota(jnp.int32, (SUB, lanes), 0)
+        at_lane = lax.broadcasted_iota(jnp.int32, (SUB, lanes), 1)
+        mine, theirs = at_lane - own * count, at_lane - (1 - own) * count
+        tile = jnp.zeros((SUB, lanes), jnp.float32)
+        sent = jnp.zeros((SUB, lanes), jnp.float32)
+        for i in range(count):
+            for k in range(kinds):
+                value = sum_ref[i, k]
+                for shift in (4, 2, 1):
+                    value = value + pltpu.roll(value, shift, 0)
+                if k < near:
+                    j = (i + k) % count
+                    here = (at_row == i) & (mine == j)
+                    if 0 < k < near - 1:
+                        here = here | ((at_row == j) & (mine == i))
+                    tile = tile + jnp.where(here, value, 0.0)
+                else:
+                    j = k - near
+                    tile = tile + jnp.where((at_row == i) & (theirs == j), value, 0.0)
+                    sent = sent + jnp.where((at_row == j) & (mine == i), value, 0.0)
+        gt_ref[0] = sent
+        gt_ref[1] = tile
+
+    def gram_round(k):
+        tile_copy(k).wait()
+        gt_ref[k + 2] = gt_ref[k + 1] + gr_ref[k]
+        if k + 1 < len(rounds):
+            tile_copy(k + 1).start()
+
+    round_ends = (7, 9, 12, 14, 17, 22)
+
+    def out_copy(p):
+        return pltpu.make_async_copy(out_ref.at[p], hessian_ref.at[p], out_sem.at[p])
+
     last = STEPS - 1
 
     def first_step(p, _):
+        pltpu.make_async_copy(inputs[0].at[p], probes_ref.at[p], load_sem.at[8 + p]).wait()
         for z in range(nz):
             for t in range(tiles):
                 s_ref[p, z, rows_of(t), :] = coef(SRC, z, t) * probes_ref[p, z, rows_of(t), :]
@@ -254,6 +413,10 @@
         return 0
 
     lax.fori_loop(0, count, first_step, 0)
+    pair_copy(0).start()
+    for k in (1, 3, 5):
+        loads[k].wait()
+    lax.fori_loop(0, nz, prepare, 0)
 
     def forward_step(i, _):
         n, p = i // count + 1, i % count
@@ -262,6 +425,15 @@
         forward(n - 1, before, p)
         finish_state(n, now, p)
         send(now, p, state_sources(n, now, p))
+
+        @pl.when(p == count - 1)
+        def _():
+            pair_copy(n).start()
+
+        @pl.when(p % 2 == 1)
+        def _():
+            gram_unit(n - 1, p - 1)
+
         return 0
 
     lax.fori_loop(0, (last - 1) * count, forward_step, 0)
@@ -276,9 +448,15 @@
         out_ref[p] = pulled
         finish_adjoint(now, p, pulled)
         send(now, p, adjoint_sources(now, p))
+
+        @pl.when(p % 2 == 1)
+        def _():
+            gram_unit(last - 1, p - 1)
+
         return 0
 
     lax.fori_loop(0, count, turn_step, 0)
+    pair_copy(last).start()
 
     def backward_step(i, _):
         k, p = i // count + 1, i % count
@@ -289,6 +467,22 @@
         out_ref[p] += pulled
         finish_adjoint(now, p, pulled)
         send(now, p, adjoint_sources(now, p))
+
+        @pl.when((i >= 2) & (i < 6))
+        def _():
+            gram_unit(last, 2 * (i - 2))
+
+        @pl.when(i == 5)
+        def _():
+            gram_tile()
+            tile_copy(0).start()
+
+        for k, end in enumerate(round_ends[: len(rounds)]):
+
+            @pl.when(i == end)
+            def _():
+                gram_round(k)
+
         return 0
 
     lax.fori_loop(0, (last - 1) * count, backward_step, 0)
@@ -298,25 +492,34 @@
         settle(before, p, adjoint_sources(before, p))
         backward(0, before, p)
         out_ref[p] = coef_ref[SRC] * (out_ref[p] + solve())
+        out_copy(p).start()
         return 0
 
     lax.fori_loop(0, count, last_step, 0)
-
-
-def by_axis(array, axes):
-    return functools.reduce(lax.psum, axes, array)
+    for k in range(len(round_ends), len(rounds)):
+        gram_round(k)
+    for p in range(count):
+        out_copy(p).wait()
+    gram_ref[...] = gt_ref[len(rounds) + 1, :, : gram_ref.shape[1]] / (nz * ny * nx * zn * yn)
 
 
 def shards(probes, velocity, prior_scale, noise_precision, source_mask, sensor_mask):
     count, nz, ny, nx = probes.shape
     high, low = implicit_matrix(nx)
-    vmem = pl.BlockSpec(memory_space=pltpu.VMEM)
-    hessian = pl.pallas_call(
+    arguments = (probes, velocity, prior_scale, noise_precision, source_mask, sensor_mask, high, low)
+    cores = lax.axis_size("pa")
+    rounds = 1 + (lax.axis_size("gy") - 1).bit_length() + (lax.axis_size("gz") - 1).bit_length()
+    near = count // 2 + 1
+    return pl.pallas_call(
         kernel,
-        out_shape=jax.ShapeDtypeStruct(probes.shape, jnp.float32),
-        in_specs=[vmem] * 8,
-        out_specs=vmem,
+        out_shape=(
+            jax.ShapeDtypeStruct(probes.shape, jnp.float32),
+            jax.ShapeDtypeStruct((count, cores * count), jnp.float32),
+        ),
+        in_specs=[pl.BlockSpec(memory_space=pltpu.HBM)] * len(arguments),
+        out_specs=(pl.BlockSpec(memory_space=pltpu.HBM), pl.BlockSpec(memory_space=pltpu.VMEM)),
         scratch_shapes=[
+            *(pltpu.VMEM(array.shape, array.dtype) for array in arguments),
             pltpu.VMEM((STEPS, count, nz, ny, nx), jnp.float32),
             pltpu.VMEM((count, nz, ny, nx), jnp.float32),
             pltpu.VMEM((count, nz, ny, nx), jnp.float32),
@@ -329,20 +532,24 @@
             pltpu.VMEM((2, 2, count, nz, nx), jnp.float32),
             pltpu.SemaphoreType.DMA((2, 4, count)),
             pltpu.SemaphoreType.DMA((2, 4, count)),
+            pltpu.SemaphoreType.DMA((8 + count,)),
+            pltpu.VMEM((count, nz, ny, nx), jnp.float32),
+            pltpu.SemaphoreType.DMA((count,)),
+            pltpu.VMEM((STEPS, count, nz // 2, ny, nx), jnp.float32),
+            pltpu.VMEM((count, near + count, SUB, 128), jnp.float32),
+            pltpu.VMEM((count, near + count, SUB, 128), jnp.float32),
+            pltpu.VMEM((rounds + 2, SUB, 128), jnp.float32),
+            pltpu.VMEM((rounds, SUB, 128), jnp.float32),
+            pltpu.SemaphoreType.DMA((STEPS,)),
+            pltpu.SemaphoreType.DMA((STEPS,)),
+            pltpu.SemaphoreType.DMA((rounds,)),
+            pltpu.SemaphoreType.DMA((rounds,)),
         ],
         compiler_params=pltpu.CompilerParams(
-            collective_id=0, has_side_effects=True, vmem_limit_bytes=48 * 1024 * 1024
+            collective_id=0, has_side_effects=True, vmem_limit_bytes=60 * 1024 * 1024
         ),
         name="solve",
-    )(probes, velocity, prior_scale, noise_precision, source_mask, sensor_mask, high, low)
-    own_rows = probes.reshape(count, -1)
-    piece = lax.all_gather(hessian, "pa", axis=0, tiled=True)
-    partial_gram = jnp.einsum(
-        "ac,bc->ab", own_rows, piece.reshape(piece.shape[0], -1), precision=lax.Precision.HIGHEST
-    )
-    total_cells = nz * ny * nx * lax.axis_size("gz") * lax.axis_size("gy")
-    gram = by_axis(partial_gram, ("gz", "gy")) / total_cells
-    return (hessian, gram)
+    )(*arguments)
 
 
 def solution(mesh):

time: 166 us -> 98.6 us (0.59)
  blocking collectives: 41.6 us -> 0 us
  Pallas kernels: 58.9 us -> 94.1 us
  waiting for transfers between devices: 31 us -> 0 us
  between operations: 14.1 us -> 0.65 us
  matrix products: 9.18 us -> 0 us
  local copies, waits for them, and re-layouts: 9.9 us -> 3.76 us
    psum x2 -> x0, blocking collectives: 41.6 us -> none  [by_axis(): return functools.reduce(lax.psum, axes, array)]
    pallas_call x1, Pallas kernels: 58.9 us -> 94.1 us  [shards(): pl.pallas_call(kernel, out_shape=(jax.ShapeDtypeStruct(probes.shape, jnp....]
    all_gather x1 -> x0, waiting for transfers between devices: 30.9 us -> none  [shards(): piece = lax.all_gather(hessian, 'pa', axis=0, tiled=True)]
    dot_general x1 -> x0, matrix products: 9.18 us -> none  [shards(): jnp.einsum('ac,bc->ab', own_rows, piece.reshape(piece.shape[0], -1), prec...]
    unnamed x17 -> x4, local copies, waits for them, and re-layouts: 9.9 us -> 3.76 us
  transfers between devices with their start and end apart: 1 -> 0, of which waited for: 1 -> 0; matrix products, arithmetic and copies ran while one was open for 0% -> 0% of each run, Pallas kernels for 0% -> 0%
where the time goes in v1:
time: 98.6 us; the launch traced here: 98.5 us
  Pallas kernels  94.1 us (95%)
  local copies, waits for them, and re-layouts  3.76 us (4%)
    pallas_call x1, Pallas kernels, shards(): pl.pallas_call(kernel, out_shape=(jax.ShapeDtypeStruct(probes.shape, jnp....  94.1 us
    unnamed x4, local copies, waits for them, and re-layouts  3.76 us

profile of v1, /device:TPU:40, one launch (start us, length us, event | category | flops | bytes accessed | tf_op | source)
XLA Modules:
  0.0 98.5 jit_solution(15895492775809440524)
XLA Ops:
  0.6 94.1 %solve.1 = (f32[8,8,32,256]{3,2,1,0:T(8,128)}, f32[8,16]{1,0:T(8,128)}) custom-call(f32[8,8,32,256]{3,2,1,0:T(8,128)} %refs_0_.1, f32[3,8,32,256]{3,2,1,0:T(8,128)} %refs_1_.1, f32[8,32,256]{2,1,0:T(8,128)} %refs_2_.1, f32[8,32,256]{2,1,0:T(8,128)} %refs_3_.1, s32[8,32,256]{2,1,0:T(8,128)} %refs_4_.1, s32[8,32,256]{2,1,0:T(8,128)} %refs_5_.1, ...), custom_call_target="tpu_custom_call" | custom-call | tf_op jit(solution)/shard_map/solve/pallas_call | solution.py:513
  94.7 0.0 copy-start
  94.7 3.2 %copy.12 = f32[8,8,32,256]{3,2,1,0:T(8,128)} copy(f32[8,8,32,256]{3,2,1,0:T(8,128)} %get-tuple-element.4) | data formatting | bytes 4194304
  97.9 0.0 copy-done
  97.9 0.6 copy.13
Async XLA Ops:
  94.7 3.2 %copy-start = (f32[8,16]{1,0:T(8,128)S(1)}, f32[8,16]{1,0:T(8,128)}, u32[]{:S(2)}) copy-start(f32[8,16]{1,0:T(8,128)} %get-tuple-element.5) | copy-start | bytes 1540

commit v2 on v1

--- a/solution.py
+++ b/solution.py
@@ -58,8 +58,14 @@
     gr_ref,
     pair_send,
     pair_recv,
-    tile_send,
-    tile_recv,
+    ys_sem,
+    yr_sem,
+    zs_sem,
+    zr_sem,
+    core_sem,
+    word_sem,
+    ytile_ref,
+    ztile_ref,
     ) = refs
     count, nz, ny, nx = probes_ref.shape
     tiles = ny // SUB
@@ -79,13 +85,11 @@
     def crossed(me, distance):
         return me + distance * (1 - 2 * ((me // distance) % 2))
 
-    rounds = [{"pa": 1 - own}]
-    for axis, me, n in (("gy", yi, yn), ("gz", zi, zn)):
-        distance = 1
-        while distance < n:
-            rounds.append({axis: crossed(me, distance)})
-            distance *= 2
-    far = 1 if zn > 8 else 0
+    def doubled(axis, me, n):
+        return [{axis: crossed(me, 1 << k)} for k in range((n - 1).bit_length())]
+
+    other_core = {"pa": 1 - own}
+    y_doubled, z_doubled = doubled("gy", yi, yn), doubled("gz", zi, zn)
     z_other = zi - 1 + 2 * (zi % 2)
     y_other = yi - 1 + 2 * (yi % 2)
     met = [
@@ -103,7 +107,7 @@
         copy.start()
 
     barrier = pltpu.get_barrier_semaphore()
-    greeted = rounds[: len(rounds) - far]
+    greeted = [other_core] + y_doubled + z_doubled[:3]
     for device in greeted:
         pl.semaphore_signal(barrier, inc=1, device_id=device, device_id_type=MESH)
     for there, device in met:
@@ -292,19 +296,71 @@
             dst_ref=pu_ref.at[n],
             send_sem=pair_send.at[n],
             recv_sem=pair_recv.at[n],
-            device_id=rounds[0],
+            device_id=other_core,
             device_id_type=MESH,
         )
 
-    def tile_copy(k):
+    def core_tile():
         return pltpu.make_async_remote_copy(
-            src_ref=gt_ref.at[k if k == 0 else k + 1],
-            dst_ref=gr_ref.at[k],
-            send_sem=tile_send.at[k],
-            recv_sem=tile_recv.at[k],
-            device_id=rounds[k],
+            src_ref=gt_ref.at[0],
+            dst_ref=gr_ref,
+            send_sem=core_sem.at[0],
+            recv_sem=core_sem.at[1],
+            device_id=other_core,
             device_id_type=MESH,
         )
+
+    def along(axis, me, n, tiles_ref, source, out_sem, in_sem):
+        def move(distance):
+            return pltpu.make_async_remote_copy(
+                src_ref=source,
+                dst_ref=tiles_ref.at[me],
+                send_sem=out_sem.at[distance],
+                recv_sem=in_sem.at[me],
+                device_id={axis: (me + distance) % n},
+                device_id_type=MESH,
+            )
+
+        def arrival(who):
+            return pltpu.make_async_remote_copy(
+                src_ref=source,
+                dst_ref=tiles_ref.at[who],
+                send_sem=out_sem.at[0],
+                recv_sem=in_sem.at[who],
+                device_id={axis: (me + 1) % n},
+                device_id_type=MESH,
+            )
+
+        def start():
+            def step(distance, _):
+                move(distance).start()
+                return 0
+
+            lax.fori_loop(1, n, step, 0)
+
+        def end():
+            def step(distance, _):
+                arrival((me + distance) % n).wait_recv()
+                move(distance).wait_send()
+                return 0
+
+            lax.fori_loop(1, n, step, 0)
+            tiles_ref[me] = source[...]
+            total = tiles_ref[0]
+            for who in range(1, n):
+                total = total + tiles_ref[who]
+            return total
+
+        return start, end
+
+    start_y, end_y = along("gy", yi, yn, ytile_ref, gt_ref.at[2], ys_sem, yr_sem)
+    start_z, end_z = along("gz", zi, zn, ztile_ref, gt_ref.at[3], zs_sem, zr_sem)
+
+    def pass_word(k):
+        if 0 < k <= len(z_doubled[:3]):
+            pl.semaphore_wait(word_sem.at[k - 1], 1)
+        if k < len(z_doubled[:3]):
+            pl.semaphore_signal(word_sem.at[k], inc=1, device_id=z_doubled[k], device_id_type=MESH)
 
     near = count // 2 + 1
     lanes = 128
@@ -319,36 +375,38 @@
         def _():
             pair_copy(n).wait()
 
-        def own_terms(z, sums):
+        def own_terms(k, sums):
             sums = list(sums)
-            for t, h in pieces:
-                where = (rows_of(t), pl.ds(h * lanes, lanes))
-                x = [u_ref[(n, (i + d) % count, z) + where] for d in range(near + 1)]
-                weight = coef_ref[(OBS, z) + where]
-                for r in range(2):
-                    scaled = weight * x[r]
-                    for d in range(near):
-                        sums[r * near + d] = sums[r * near + d] + scaled * x[r + d]
+            for z in (2 * k, 2 * k + 1):
+                for t, h in pieces:
+                    where = (rows_of(t), pl.ds(h * lanes, lanes))
+                    x = [u_ref[(n, (i + d) % count, z) + where] for d in range(near + 1)]
+                    weight = coef_ref[(OBS, z) + where]
+                    for r in range(2):
+                        scaled = weight * x[r]
+                        for d in range(near):
+                            sums[r * near + d] = sums[r * near + d] + scaled * x[r + d]
             return tuple(sums)
 
-        def pair_terms(z, sums):
+        def pair_terms(k, sums):
             sums = list(sums)
-            for t, h in pieces:
-                where = (rows_of(t), pl.ds(h * lanes, lanes))
-                weight = coef_ref[(OBS, own * half + z) + where]
-                scaled = [weight * u_ref[(n, i + r, own * half + z) + where] for r in range(2)]
-                for j in range(count):
-                    y = pu_ref[(n, j, z) + where]
-                    for r in range(2):
-                        sums[r * count + j] = sums[r * count + j] + scaled[r] * y
+            for z in (2 * k, 2 * k + 1):
+                for t, h in pieces:
+                    where = (rows_of(t), pl.ds(h * lanes, lanes))
+                    weight = coef_ref[(OBS, own * half + z) + where]
+                    scaled = [weight * u_ref[(n, i + r, own * half + z) + where] for r in range(2)]
+                    for j in range(count):
+                        y = pu_ref[(n, j, z) + where]
+                        for r in range(2):
+                            sums[r * count + j] = sums[r * count + j] + scaled[r] * y
             return tuple(sums)
 
         zero = jnp.zeros((SUB, lanes), jnp.float32)
-        sums = lax.fori_loop(0, nz, own_terms, (zero,) * (2 * near))
+        sums = lax.fori_loop(0, nz // 2, own_terms, (zero,) * (2 * near))
         for r in range(2):
             for d in range(near):
                 acc_ref[i + r, d] += sums[r * near + d]
-        sums = lax.fori_loop(0, half, pair_terms, (zero,) * (2 * count))
+        sums = lax.fori_loop(0, half // 2, pair_terms, (zero,) * (2 * count))
         for r in range(2):
             for j in range(count):
                 acc_ref[i + r, near + j] += sums[r * count + j]
@@ -389,13 +447,14 @@
         gt_ref[0] = sent
         gt_ref[1] = tile
 
-    def gram_round(k):
-        tile_copy(k).wait()
-        gt_ref[k + 2] = gt_ref[k + 1] + gr_ref[k]
-        if k + 1 < len(rounds):
-            tile_copy(k + 1).start()
-
-    round_ends = (7, 9, 12, 14, 17, 22)
+    def end_core():
+        core_tile().wait()
+        gt_ref[2] = gt_ref[1] + gr_ref[...]
+        start_y()
+
+    def end_rows():
+        gt_ref[3] = end_y()
+        start_z()
 
     def out_copy(p):
         return pltpu.make_async_copy(out_ref.at[p], hessian_ref.at[p], out_sem.at[p])
@@ -457,6 +516,7 @@
 
     lax.fori_loop(0, count, turn_step, 0)
     pair_copy(last).start()
+    pass_word(0)
 
     def backward_step(i, _):
         k, p = i // count + 1, i % count
@@ -472,17 +532,19 @@
         def _():
             gram_unit(last, 2 * (i - 2))
 
+        for k, when in enumerate((1, 4, 8)):
+
+            @pl.when(i == when)
+            def _():
+                pass_word(k + 1)
+
         @pl.when(i == 5)
         def _():
             gram_tile()
-            tile_copy(0).start()
-
-        for k, end in enumerate(round_ends[: len(rounds)]):
-
-            @pl.when(i == end)
-            def _():
-                gram_round(k)
-
+            core_tile().start()
+
+        pl.when(i == 7)(end_core)
+        pl.when(i == 10)(end_rows)
         return 0
 
     lax.fori_loop(0, (last - 1) * count, backward_step, 0)
@@ -496,11 +558,9 @@
         return 0
 
     lax.fori_loop(0, count, last_step, 0)
-    for k in range(len(round_ends), len(rounds)):
-        gram_round(k)
     for p in range(count):
         out_copy(p).wait()
-    gram_ref[...] = gt_ref[len(rounds) + 1, :, : gram_ref.shape[1]] / (nz * ny * nx * zn * yn)
+    gram_ref[...] = end_z()[:, : gram_ref.shape[1]] / (nz * ny * nx * zn * yn)
 
 
 def shards(probes, velocity, prior_scale, noise_precision, source_mask, sensor_mask):
@@ -508,7 +568,7 @@
     high, low = implicit_matrix(nx)
     arguments = (probes, velocity, prior_scale, noise_precision, source_mask, sensor_mask, high, low)
     cores = lax.axis_size("pa")
-    rounds = 1 + (lax.axis_size("gy") - 1).bit_length() + (lax.axis_size("gz") - 1).bit_length()
+    zn, yn = lax.axis_size("gz"), lax.axis_size("gy")
     near = count // 2 + 1
     return pl.pallas_call(
         kernel,
@@ -538,12 +598,18 @@
             pltpu.VMEM((STEPS, count, nz // 2, ny, nx), jnp.float32),
             pltpu.VMEM((count, near + count, SUB, 128), jnp.float32),
             pltpu.VMEM((count, near + count, SUB, 128), jnp.float32),
-            pltpu.VMEM((rounds + 2, SUB, 128), jnp.float32),
-            pltpu.VMEM((rounds, SUB, 128), jnp.float32),
+            pltpu.VMEM((4, SUB, 128), jnp.float32),
+            pltpu.VMEM((SUB, 128), jnp.float32),
             pltpu.SemaphoreType.DMA((STEPS,)),
             pltpu.SemaphoreType.DMA((STEPS,)),
-            pltpu.SemaphoreType.DMA((rounds,)),
-            pltpu.SemaphoreType.DMA((rounds,)),
+            pltpu.SemaphoreType.DMA((yn,)),
+            pltpu.SemaphoreType.DMA((yn,)),
+            pltpu.SemaphoreType.DMA((zn,)),
+            pltpu.SemaphoreType.DMA((zn,)),
+            pltpu.SemaphoreType.DMA((2,)),
+            pltpu.SemaphoreType.REGULAR((3,)),
+            pltpu.VMEM((yn, SUB, 128), jnp.float32),
+            pltpu.VMEM((zn, SUB, 128), jnp.float32),
         ],
         compiler_params=pltpu.CompilerParams(
             collective_id=0, has_side_effects=True, vmem_limit_bytes=60 * 1024 * 1024

time: 98.6 us -> 88.3 us (0.90)
  the two profiles are of different devices: /device:TPU:40 before, /device:TPU:33 now
where the time goes in v2:
time: 88.3 us; the launch traced here: 88.2 us
  Pallas kernels  83.8 us (95%)
  local copies, waits for them, and re-layouts  3.76 us (4%)
    pallas_call x1, Pallas kernels, shards(): pl.pallas_call(kernel, out_shape=(jax.ShapeDtypeStruct(probes.shape, jnp....  83.8 us
    unnamed x4, local copies, waits for them, and re-layouts  3.76 us

profile of v2, /device:TPU:33, one launch (start us, length us, event | category | flops | bytes accessed | tf_op | source)
XLA Modules:
  0.0 88.2 jit_solution(15565098129749775582)
XLA Ops:
  0.6 83.8 %solve.1 = (f32[8,8,32,256]{3,2,1,0:T(8,128)}, f32[8,16]{1,0:T(8,128)}) custom-call(f32[8,8,32,256]{3,2,1,0:T(8,128)} %refs_0_.1, f32[3,8,32,256]{3,2,1,0:T(8,128)} %refs_1_.1, f32[8,32,256]{2,1,0:T(8,128)} %refs_2_.1, f32[8,32,256]{2,1,0:T(8,128)} %refs_3_.1, s32[8,32,256]{2,1,0:T(8,128)} %refs_4_.1, s32[8,32,256]{2,1,0:T(8,128)} %refs_5_.1, ...), custom_call_target="tpu_custom_call" | custom-call | tf_op jit(solution)/shard_map/solve/pallas_call | solution.py:573
  84.4 0.0 copy-start
  84.4 3.2 %copy.12 = f32[8,8,32,256]{3,2,1,0:T(8,128)} copy(f32[8,8,32,256]{3,2,1,0:T(8,128)} %get-tuple-element.4) | data formatting | bytes 4194304
  87.6 0.0 copy-done
  87.6 0.6 copy.13
Async XLA Ops:
  84.4 3.2 %copy-start = (f32[8,16]{1,0:T(8,128)S(1)}, f32[8,16]{1,0:T(8,128)}, u32[]{:S(2)}) copy-start(f32[8,16]{1,0:T(8,128)} %get-tuple-element.5) | copy-start | bytes 1540

commit v3 on v2

--- a/solution.py
+++ b/solution.py
@@ -155,28 +155,28 @@
     loads[7].wait()
     pl.semaphore_wait(barrier, len(greeted) + sum(there.astype(jnp.int32) for there, _ in met))
 
-    def copies(slot, p, sources):
+    def copies(slot, q, sources):
         result = []
         for side in range(4):
             halo = zh_ref if side < 2 else yh_ref
             result.append(
                 pltpu.make_async_remote_copy(
                     src_ref=sources[side],
-                    dst_ref=halo.at[slot, (side % 2) ^ 1, p],
-                    send_sem=send_sem.at[slot, side, p],
-                    recv_sem=recv_sem.at[slot, side ^ 1, p],
+                    dst_ref=halo.at[slot, (side % 2) ^ 1, pl.ds(2 * q, 2)],
+                    send_sem=send_sem.at[slot, side, q],
+                    recv_sem=recv_sem.at[slot, side ^ 1, q],
                     device_id=target[side],
                     device_id_type=MESH,
                 )
             )
         return result
 
-    def send(slot, p, sources):
-        for side, copy in enumerate(copies(slot, p, sources)):
+    def send(slot, q, sources):
+        for side, copy in enumerate(copies(slot, q, sources)):
             pl.when(exists[side])(copy.start)
 
-    def settle(slot, p, sources):
-        moved = copies(slot, p, sources)
+    def settle(slot, q, sources):
+        moved = copies(slot, q, sources)
         for side in range(4):
 
             @pl.when(exists[side])
@@ -184,30 +184,36 @@
                 moved[side ^ 1].wait_recv()
                 moved[side].wait_send()
 
-    def state_sources(n, slot, p):
-        return [u_ref.at[n, p, 0], u_ref.at[n, p, nz - 1], ys_ref.at[slot, 0, p], ys_ref.at[slot, 1, p]]
-
-    def adjoint_sources(slot, p):
-        return [zs_ref.at[slot, 0, p], zs_ref.at[slot, 1, p], ys_ref.at[slot, 0, p], ys_ref.at[slot, 1, p]]
-
-    def put(z, pair, left, right):
+    def state_sources(n, slot, q):
+        two = pl.ds(2 * q, 2)
+        return [u_ref.at[n, two, 0], u_ref.at[n, two, nz - 1], ys_ref.at[slot, 0, two], ys_ref.at[slot, 1, two]]
+
+    def adjoint_sources(slot, q):
+        return [source.at[slot, side, pl.ds(2 * q, 2)] for source in (zs_ref, ys_ref) for side in range(2)]
+
+    def both(q, *parts):
+        for part in parts:
+            for r in range(2):
+                part(r, 2 * q + r)
+
+    def put(r, z, pair, left, right):
         rows = jnp.concatenate([left, right], axis=0)
         high = rows.astype(jnp.bfloat16)
         low = (rows - high.astype(jnp.float32)).astype(jnp.bfloat16)
         where = pl.ds(z * ny + pair * 2 * SUB, 2 * SUB)
-        whi_ref[where, :] = high
-        wlo_ref[where, :] = low
-
-    def solve():
+        whi_ref[r, where, :] = high
+        wlo_ref[r, where, :] = low
+
+    def solve(r):
         dot = functools.partial(jnp.dot, preferred_element_type=jnp.float32)
-        high, low = whi_ref[...], wlo_ref[...]
+        high, low = whi_ref[r], wlo_ref[r]
         moved = dot(high, mhi_ref[...]) + (dot(high, mlo_ref[...]) + dot(low, mhi_ref[...]))
         return moved.reshape(nz, ny, nx)
 
-    def by_tile(make):
+    def by_tile(r, make):
         for z in range(nz):
             for pair in range(tiles // 2):
-                put(z, pair, make(z, 2 * pair), make(z, 2 * pair + 1))
+                put(r, z, pair, make(z, 2 * pair), make(z, 2 * pair + 1))
 
     def rows_of(t):
         return pl.ds(t * SUB, SUB)
@@ -215,7 +221,7 @@
     def coef(kind, z, t):
         return coef_ref[kind, z, rows_of(t), :]
 
-    def forward(n, slot, p):
+    def forward(r, n, slot, p):
         def make(z, t):
             def at(zz, tt):
                 return u_ref[n, p, zz, rows_of(tt), :]
@@ -240,9 +246,9 @@
                 coef(CXP, z, t) * pltpu.roll(centre, nx - 1, 1) + coef(CXM, z, t) * pltpu.roll(centre, 1, 1)
             )
 
-        by_tile(make)
-
-    def backward(n, slot, p):
+        by_tile(r, make)
+
+    def backward(r, n, slot, p):
         def make(z, t):
             def at(zz, tt):
                 return b_ref[p, zz, rows_of(tt), :]
@@ -273,10 +279,10 @@
                 pltpu.roll(coef(CXM, z, t) * centre, nx - 1, 1) + pltpu.roll(coef(CXP, z, t) * centre, 1, 1)
             )
 
-        by_tile(make)
-
-    def finish_state(n, slot, p):
-        state = solve()
+        by_tile(r, make)
+
+    def finish_state(r, n, slot, p):
+        state = solve(r)
         u_ref[n, p] = state
         for z in range(nz):
             ys_ref[slot, 0, p, pl.ds(z, 1), :] = state[z, 0:1, :]
@@ -461,103 +467,117 @@
 
     last = STEPS - 1
 
-    def first_step(p, _):
-        pltpu.make_async_copy(inputs[0].at[p], probes_ref.at[p], load_sem.at[8 + p]).wait()
-        for z in range(nz):
-            for t in range(tiles):
-                s_ref[p, z, rows_of(t), :] = coef(SRC, z, t) * probes_ref[p, z, rows_of(t), :]
-        by_tile(lambda z, t: coef(SRC, z, t) * probes_ref[p, z, rows_of(t), :])
-        finish_state(0, 0, p)
-        send(0, p, state_sources(0, 0, p))
+    pairs = count // 2
+
+    def first_step(q, _):
+        def source(r, p):
+            pltpu.make_async_copy(inputs[0].at[p], probes_ref.at[p], load_sem.at[8 + p]).wait()
+            for z in range(nz):
+                for t in range(tiles):
+                    s_ref[p, z, rows_of(t), :] = coef(SRC, z, t) * probes_ref[p, z, rows_of(t), :]
+            by_tile(r, lambda z, t: coef(SRC, z, t) * probes_ref[p, z, rows_of(t), :])
+
+        both(q, source, lambda r, p: finish_state(r, 0, 0, p))
+        send(0, q, state_sources(0, 0, q))
         return 0
 
-    lax.fori_loop(0, count, first_step, 0)
+    lax.fori_loop(0, pairs, first_step, 0)
     pair_copy(0).start()
     for k in (1, 3, 5):
         loads[k].wait()
     lax.fori_loop(0, nz, prepare, 0)
 
     def forward_step(i, _):
-        n, p = i // count + 1, i % count
+        n, q = i // pairs + 1, i % pairs
         before, now = (n + 1) % 2, n % 2
-        settle(before, p, state_sources(n - 1, before, p))
-        forward(n - 1, before, p)
-        finish_state(n, now, p)
-        send(now, p, state_sources(n, now, p))
-
-        @pl.when(p == count - 1)
+        settle(before, q, state_sources(n - 1, before, q))
+        both(
+            q,
+            lambda r, p: forward(r, n - 1, before, p),
+            lambda r, p: finish_state(r, n, now, p),
+        )
+        send(now, q, state_sources(n, now, q))
+
+        @pl.when(q == pairs - 1)
         def _():
             pair_copy(n).start()
 
-        @pl.when(p % 2 == 1)
-        def _():
-            gram_unit(n - 1, p - 1)
-
+        gram_unit(n - 1, 2 * q)
         return 0
 
-    lax.fori_loop(0, (last - 1) * count, forward_step, 0)
-
-    def turn_step(p, _):
+    lax.fori_loop(0, (last - 1) * pairs, forward_step, 0)
+
+    def turn_step(q, _):
         before, now = (last + 1) % 2, last % 2
-        settle(before, p, state_sources(last - 1, before, p))
-        forward(last - 1, before, p)
-        u_ref[last, p] = solve()
-        by_tile(lambda z, t: coef(OBS, z, t) * u_ref[last, p, z, rows_of(t), :])
-        pulled = solve()
-        out_ref[p] = pulled
-        finish_adjoint(now, p, pulled)
-        send(now, p, adjoint_sources(now, p))
-
-        @pl.when(p % 2 == 1)
-        def _():
-            gram_unit(last - 1, p - 1)
-
+        settle(before, q, state_sources(last - 1, before, q))
+
+        def turn(r, p):
+            u_ref[last, p] = solve(r)
+            by_tile(r, lambda z, t: coef(OBS, z, t) * u_ref[last, p, z, rows_of(t), :])
+
+        def pull(r, p):
+            pulled = solve(r)
+            out_ref[p] = pulled
+            finish_adjoint(now, p, pulled)
+
+        both(q, lambda r, p: forward(r, last - 1, before, p), turn, pull)
+        send(now, q, adjoint_sources(now, q))
+        gram_unit(last - 1, 2 * q)
         return 0
 
-    lax.fori_loop(0, count, turn_step, 0)
+    lax.fori_loop(0, pairs, turn_step, 0)
     pair_copy(last).start()
     pass_word(0)
 
     def backward_step(i, _):
-        k, p = i // count + 1, i % count
+        k, q = i // pairs + 1, i % pairs
         before, now = (last + k + 1) % 2, (last + k) % 2
-        settle(before, p, adjoint_sources(before, p))
-        backward(last - k, before, p)
-        pulled = solve()
-        out_ref[p] += pulled
-        finish_adjoint(now, p, pulled)
-        send(now, p, adjoint_sources(now, p))
-
-        @pl.when((i >= 2) & (i < 6))
-        def _():
-            gram_unit(last, 2 * (i - 2))
-
-        for k, when in enumerate((1, 4, 8)):
+        settle(before, q, adjoint_sources(before, q))
+
+        def pull(r, p):
+            pulled = solve(r)
+            out_ref[p] += pulled
+            finish_adjoint(now, p, pulled)
+
+        both(q, lambda r, p: backward(r, last - k, before, p), pull)
+        send(now, q, adjoint_sources(now, q))
+
+        for turn, when in enumerate((0, 2, 4)):
 
             @pl.when(i == when)
             def _():
-                pass_word(k + 1)
-
-        @pl.when(i == 5)
+                pass_word(turn + 1)
+
+        @pl.when((i >= 1) & (i < 3))
+        def _():
+            def unit(r, _):
+                gram_unit(last, 4 * (i - 1) + 2 * r)
+                return 0
+
+            lax.fori_loop(0, 2, unit, 0)
+
+        @pl.when(i == 2)
         def _():
             gram_tile()
             core_tile().start()
 
-        pl.when(i == 7)(end_core)
-        pl.when(i == 10)(end_rows)
+        pl.when(i == 3)(end_core)
+        pl.when(i == 5)(end_rows)
         return 0
 
-    lax.fori_loop(0, (last - 1) * count, backward_step, 0)
-
-    def last_step(p, _):
+    lax.fori_loop(0, (last - 1) * pairs, backward_step, 0)
+
+    def last_step(q, _):
         before = (2 * last + 1) % 2
-        settle(before, p, adjoint_sources(before, p))
-        backward(0, before, p)
-        out_ref[p] = coef_ref[SRC] * (out_ref[p] + solve())
-        out_copy(p).start()
+        settle(before, q, adjoint_sources(before, q))
+
+        def pull(r, p):
+            out_ref[p] = coef_ref[SRC] * (out_ref[p] + solve(r))
+
+        both(q, lambda r, p: backward(r, 0, before, p), pull, lambda r, p: out_copy(p).start())
         return 0
 
-    lax.fori_loop(0, count, last_step, 0)
+    lax.fori_loop(0, pairs, last_step, 0)
     for p in range(count):
         out_copy(p).wait()
     gram_ref[...] = end_z()[:, : gram_ref.shape[1]] / (nz * ny * nx * zn * yn)
@@ -584,14 +604,14 @@
             pltpu.VMEM((count, nz, ny, nx), jnp.float32),
             pltpu.VMEM((count, nz, ny, nx), jnp.float32),
             pltpu.VMEM((8, nz, ny, nx), jnp.float32),
-            pltpu.VMEM((nz * ny, nx), jnp.bfloat16),
-            pltpu.VMEM((nz * ny, nx), jnp.bfloat16),
+            pltpu.VMEM((2, nz * ny, nx), jnp.bfloat16),
+            pltpu.VMEM((2, nz * ny, nx), jnp.bfloat16),
             pltpu.VMEM((2, 2, count, ny, nx), jnp.float32),
             pltpu.VMEM((2, 2, count, nz, nx), jnp.float32),
             pltpu.VMEM((2, 2, count, ny, nx), jnp.float32),
             pltpu.VMEM((2, 2, count, nz, nx), jnp.float32),
-            pltpu.SemaphoreType.DMA((2, 4, count)),
-            pltpu.SemaphoreType.DMA((2, 4, count)),
+            pltpu.SemaphoreType.DMA((2, 4, count // 2)),
+            pltpu.SemaphoreType.DMA((2, 4, count // 2)),
             pltpu.SemaphoreType.DMA((8 + count,)),
             pltpu.VMEM((count, nz, ny, nx), jnp.float32),
             pltpu.SemaphoreType.DMA((count,)),

time: 88.3 us -> 84 us (0.951)
  Pallas kernels: 83.8 us -> 79.5 us
    pallas_call x1, Pallas kernels: 83.8 us -> 79.5 us  [shards(): pl.pallas_call(kernel, out_shape=(jax.ShapeDtypeStruct(probes.shape, jnp....]
where the time goes in v3:
time: 84 us; the launch traced here: 83.9 us
  Pallas kernels  79.5 us (95%)
  local copies, waits for them, and re-layouts  3.76 us (4%)
    pallas_call x1, Pallas kernels, shards(): pl.pallas_call(kernel, out_shape=(jax.ShapeDtypeStruct(probes.shape, jnp....  79.5 us
    unnamed x4, local copies, waits for them, and re-layouts  3.76 us

profile of v3, /device:TPU:33, one launch (start us, length us, event | category | flops | bytes accessed | tf_op | source)
XLA Modules:
  0.0 83.9 jit_solution(2223954723860755577)
XLA Ops:
  0.6 79.5 %solve.1 = (f32[8,8,32,256]{3,2,1,0:T(8,128)}, f32[8,16]{1,0:T(8,128)}) custom-call(f32[8,8,32,256]{3,2,1,0:T(8,128)} %refs_0_.1, f32[3,8,32,256]{3,2,1,0:T(8,128)} %refs_1_.1, f32[8,32,256]{2,1,0:T(8,128)} %refs_2_.1, f32[8,32,256]{2,1,0:T(8,128)} %refs_3_.1, s32[8,32,256]{2,1,0:T(8,128)} %refs_4_.1, s32[8,32,256]{2,1,0:T(8,128)} %refs_5_.1, ...), custom_call_target="tpu_custom_call" | custom-call | tf_op jit(solution)/shard_map/solve/pallas_call | solution.py:593
  80.1 0.0 copy-start
  80.1 3.2 %copy.12 = f32[8,8,32,256]{3,2,1,0:T(8,128)} copy(f32[8,8,32,256]{3,2,1,0:T(8,128)} %get-tuple-element.4) | data formatting | bytes 4194304
  83.3 0.0 copy-done
  83.3 0.6 copy.13
Async XLA Ops:
  80.1 3.2 %copy-start = (f32[8,16]{1,0:T(8,128)S(1)}, f32[8,16]{1,0:T(8,128)}, u32[]{:S(2)}) copy-start(f32[8,16]{1,0:T(8,128)} %get-tuple-element.5) | copy-start | bytes 1540

commit v4 on v3

--- a/solution.py
+++ b/solution.py
@@ -147,7 +147,6 @@
     def _():
         yh_ref[:, 1] = jnp.zeros(yh_ref.shape[:1] + yh_ref.shape[2:], jnp.float32)
 
-    acc_ref[...] = jnp.zeros(acc_ref.shape, jnp.float32)
     loads[2].wait()
     loads[4].wait()
     coef_ref[SRC] = smask_ref[...].astype(jnp.float32) * prior_ref[...]
@@ -417,6 +416,13 @@
             for j in range(count):
                 acc_ref[i + r, near + j] += sums[r * count + j]
 
+    def gram_units(n, first, units):
+        def unit(k, _):
+            gram_unit(n, 2 * (first + k))
+            return 0
+
+        lax.fori_loop(0, units, unit, 0)
+
     def gram_tile():
         ones = jnp.ones((lanes, lanes), jnp.float32)
         kinds = near + count
@@ -483,6 +489,7 @@
 
     lax.fori_loop(0, pairs, first_step, 0)
     pair_copy(0).start()
+    acc_ref[...] = jnp.zeros(acc_ref.shape, jnp.float32)
     for k in (1, 3, 5):
         loads[k].wait()
     lax.fori_loop(0, nz, prepare, 0)
@@ -501,8 +508,8 @@
         @pl.when(q == pairs - 1)
         def _():
             pair_copy(n).start()
-
-        gram_unit(n - 1, 2 * q)
+            gram_units(n - 1, 0, pairs)
+
         return 0
 
     lax.fori_loop(0, (last - 1) * pairs, forward_step, 0)
@@ -522,12 +529,12 @@
 
         both(q, lambda r, p: forward(r, last - 1, before, p), turn, pull)
         send(now, q, adjoint_sources(now, q))
-        gram_unit(last - 1, 2 * q)
         return 0
 
     lax.fori_loop(0, pairs, turn_step, 0)
     pair_copy(last).start()
     pass_word(0)
+    gram_units(last - 1, 0, pairs)
 
     def backward_step(i, _):
         k, q = i // pairs + 1, i % pairs
@@ -550,11 +557,7 @@
 
         @pl.when((i >= 1) & (i < 3))
         def _():
-            def unit(r, _):
-                gram_unit(last, 4 * (i - 1) + 2 * r)
-                return 0
-
-            lax.fori_loop(0, 2, unit, 0)
+            gram_units(last, 2 * (i - 1), 2)
 
         @pl.when(i == 2)
         def _():
@@ -581,6 +584,21 @@
     for p in range(count):
         out_copy(p).wait()
     gram_ref[...] = end_z()[:, : gram_ref.shape[1]] / (nz * ny * nx * zn * yn)
+
+
+def hand_over(solved_ref, summed_ref, hessian_ref, gram_ref, probe_ref, tile_ref, sem):
+    count = solved_ref.shape[0]
+    moves = [(solved_ref.at[p], probe_ref.at[p], hessian_ref.at[p]) for p in range(count)]
+    moves.append((summed_ref, tile_ref, gram_ref))
+    takes = [pltpu.make_async_copy(a, b, sem.at[0, k]) for k, (a, b, _) in enumerate(moves)]
+    gives = [pltpu.make_async_copy(b, c, sem.at[1, k]) for k, (_, b, c) in enumerate(moves)]
+    for take in takes:
+        take.start()
+    for take, give in zip(takes, gives):
+        take.wait()
+        give.start()
+    for give in gives:
+        give.wait()
 
 
 def shards(probes, velocity, prior_scale, noise_precision, source_mask, sensor_mask):
@@ -590,7 +608,7 @@
     cores = lax.axis_size("pa")
     zn, yn = lax.axis_size("gz"), lax.axis_size("gy")
     near = count // 2 + 1
-    return pl.pallas_call(
+    solved, summed = pl.pallas_call(
         kernel,
         out_shape=(
             jax.ShapeDtypeStruct(probes.shape, jnp.float32),
@@ -636,6 +654,22 @@
         ),
         name="solve",
     )(*arguments)
+    return pl.pallas_call(
+        hand_over,
+        out_shape=(
+            jax.ShapeDtypeStruct(probes.shape, jnp.float32),
+            jax.ShapeDtypeStruct((count, cores * count), jnp.float32),
+        ),
+        in_specs=[pl.BlockSpec(memory_space=pltpu.HBM)] * 2,
+        out_specs=(pl.BlockSpec(memory_space=pltpu.HBM),) * 2,
+        scratch_shapes=[
+            pltpu.VMEM(probes.shape, jnp.float32),
+            pltpu.VMEM((count, cores * count), jnp.float32),
+            pltpu.SemaphoreType.DMA((2, count + 1)),
+        ],
+        compiler_params=pltpu.CompilerParams(vmem_limit_bytes=60 * 1024 * 1024),
+        name="hand_over",
+    )(solved, summed)
 
 
 def solution(mesh):

time: 84 us -> 81.2 us (0.967)
  local copies, waits for them, and re-layouts: 3.76 us -> 0 us
  Pallas kernels: 79.5 us -> 80.5 us
    unnamed x4 -> x0, local copies, waits for them, and re-layouts: 3.76 us -> none
    pallas_call x0 -> x1, Pallas kernels: none -> 2.42 us  [shards(): pl.pallas_call(hand_over, out_shape=(jax.ShapeDtypeStruct(probes.shape, j...]
    pallas_call x1, Pallas kernels: 79.5 us -> 78 us  [shards(): pl.pallas_call(kernel, out_shape=(jax.ShapeDtypeStruct(probes.shape, jnp....]
where the time goes in v4:
time: 81.2 us; the launch traced here: 81.1 us
  Pallas kernels  80.5 us (99%)
    pallas_call x1, Pallas kernels, shards(): pl.pallas_call(kernel, out_shape=(jax.ShapeDtypeStruct(probes.shape, jnp....  78 us
    pallas_call x1, Pallas kernels, shards(): pl.pallas_call(hand_over, out_shape=(jax.ShapeDtypeStruct(probes.shape, j...  2.42 us

profile of v4, /device:TPU:33, one launch (start us, length us, event | category | flops | bytes accessed | tf_op | source)
XLA Modules:
  0.0 81.1 jit_solution(13069450692540478801)
XLA Ops:
  0.6 78.0 %solve.1 = (f32[8,8,32,256]{3,2,1,0:T(8,128)}, f32[8,16]{1,0:T(8,128)}) custom-call(f32[8,8,32,256]{3,2,1,0:T(8,128)} %refs_0_.1, f32[3,8,32,256]{3,2,1,0:T(8,128)} %refs_1_.1, f32[8,32,256]{2,1,0:T(8,128)} %refs_2_.1, f32[8,32,256]{2,1,0:T(8,128)} %refs_3_.1, s32[8,32,256]{2,1,0:T(8,128)} %refs_4_.1, s32[8,32,256]{2,1,0:T(8,128)} %refs_5_.1, ...), custom_call_target="tpu_custom_call" | custom-call | tf_op jit(solution)/shard_map/solve/pallas_call | solution.py:611
  78.7 2.4 %hand_over.1 = (f32[8,8,32,256]{3,2,1,0:T(8,128)}, f32[8,16]{1,0:T(8,128)}) custom-call(f32[8,8,32,256]{3,2,1,0:T(8,128)} %get-tuple-element.4.solved_ref, f32[8,16]{1,0:T(8,128)} %get-tuple-element.5.summed_ref), custom_call_target="tpu_custom_call" | custom-call | tf_op jit(solution)/shard_map/hand_over/pallas_call | solution.py:657

commit v5 on v4

--- a/solution.py
+++ b/solution.py
@@ -549,23 +549,23 @@
         both(q, lambda r, p: backward(r, last - k, before, p), pull)
         send(now, q, adjoint_sources(now, q))
 
-        for turn, when in enumerate((0, 2, 4)):
+        for turn, when in enumerate((0, 1, 3)):
 
             @pl.when(i == when)
             def _():
                 pass_word(turn + 1)
 
-        @pl.when((i >= 1) & (i < 3))
+        @pl.when(i < 2)
         def _():
-            gram_units(last, 2 * (i - 1), 2)
-
-        @pl.when(i == 2)
+            gram_units(last, 2 * i, 2)
+
+        @pl.when(i == 1)
         def _():
             gram_tile()
             core_tile().start()
 
-        pl.when(i == 3)(end_core)
-        pl.when(i == 5)(end_rows)
+        pl.when(i == 2)(end_core)
+        pl.when(i == 4)(end_rows)
         return 0
 
     lax.fori_loop(0, (last - 1) * pairs, backward_step, 0)

time: 81.2 us -> 81.7 us (level)
  no operation moved by 1% of the time
where the time goes in v5:
time: 81.7 us; the launch traced here: 81.6 us
  Pallas kernels  81 us (99%)
    pallas_call x1, Pallas kernels, shards(): pl.pallas_call(kernel, out_shape=(jax.ShapeDtypeStruct(probes.shape, jnp....  78.5 us
    pallas_call x1, Pallas kernels, shards(): pl.pallas_call(hand_over, out_shape=(jax.ShapeDtypeStruct(probes.shape, j...  2.42 us

profile of v5, /device:TPU:33, one launch (start us, length us, event | category | flops | bytes accessed | tf_op | source)
XLA Modules:
  0.0 81.6 jit_solution(7062533194830658184)
XLA Ops:
  0.6 78.5 %solve.1 = (f32[8,8,32,256]{3,2,1,0:T(8,128)}, f32[8,16]{1,0:T(8,128)}) custom-call(f32[8,8,32,256]{3,2,1,0:T(8,128)} %refs_0_.1, f32[3,8,32,256]{3,2,1,0:T(8,128)} %refs_1_.1, f32[8,32,256]{2,1,0:T(8,128)} %refs_2_.1, f32[8,32,256]{2,1,0:T(8,128)} %refs_3_.1, s32[8,32,256]{2,1,0:T(8,128)} %refs_4_.1, s32[8,32,256]{2,1,0:T(8,128)} %refs_5_.1, ...), custom_call_target="tpu_custom_call" | custom-call | tf_op jit(solution)/shard_map/solve/pallas_call | solution.py:611
  79.2 2.4 %hand_over.1 = (f32[8,8,32,256]{3,2,1,0:T(8,128)}, f32[8,16]{1,0:T(8,128)}) custom-call(f32[8,8,32,256]{3,2,1,0:T(8,128)} %get-tuple-element.4.solved_ref, f32[8,16]{1,0:T(8,128)} %get-tuple-element.5.summed_ref), custom_call_target="tpu_custom_call" | custom-call | tf_op jit(solution)/shard_map/hand_over/pallas_call | solution.py:657

commit v6 on v4

--- a/solution.py
+++ b/solution.py
@@ -534,7 +534,6 @@
     lax.fori_loop(0, pairs, turn_step, 0)
     pair_copy(last).start()
     pass_word(0)
-    gram_units(last - 1, 0, pairs)
 
     def backward_step(i, _):
         k, q = i // pairs + 1, i % pairs
@@ -555,16 +554,16 @@
             def _():
                 pass_word(turn + 1)
 
-        @pl.when((i >= 1) & (i < 3))
+        @pl.when(i < 4)
         def _():
-            gram_units(last, 2 * (i - 1), 2)
-
-        @pl.when(i == 2)
+            gram_units(last - 1 + i // 2, 2 * (i % 2), 2)
+
+        @pl.when(i == 3)
         def _():
             gram_tile()
             core_tile().start()
 
-        pl.when(i == 3)(end_core)
+        pl.when(i == 4)(end_core)
         pl.when(i == 5)(end_rows)
         return 0
 

time: 81.2 us -> 80 us (0.985)
  Pallas kernels: 80.5 us -> 79.1 us
    pallas_call x1, Pallas kernels: 78 us -> 76.7 us  [shards(): pl.pallas_call(kernel, out_shape=(jax.ShapeDtypeStruct(probes.shape, jnp....]
where the time goes in v6:
time: 80 us; the launch traced here: 79.7 us
  Pallas kernels  79.1 us (99%)
    pallas_call x1, Pallas kernels, shards(): pl.pallas_call(kernel, out_shape=(jax.ShapeDtypeStruct(probes.shape, jnp....  76.7 us
    pallas_call x1, Pallas kernels, shards(): pl.pallas_call(hand_over, out_shape=(jax.ShapeDtypeStruct(probes.shape, j...  2.42 us

profile of v6, /device:TPU:33, one launch (start us, length us, event | category | flops | bytes accessed | tf_op | source)
XLA Modules:
  0.0 79.7 jit_solution(14922285707825550531)
XLA Ops:
  0.6 76.7 %solve.1 = (f32[8,8,32,256]{3,2,1,0:T(8,128)}, f32[8,16]{1,0:T(8,128)}) custom-call(f32[8,8,32,256]{3,2,1,0:T(8,128)} %refs_0_.1, f32[3,8,32,256]{3,2,1,0:T(8,128)} %refs_1_.1, f32[8,32,256]{2,1,0:T(8,128)} %refs_2_.1, f32[8,32,256]{2,1,0:T(8,128)} %refs_3_.1, s32[8,32,256]{2,1,0:T(8,128)} %refs_4_.1, s32[8,32,256]{2,1,0:T(8,128)} %refs_5_.1, ...), custom_call_target="tpu_custom_call" | custom-call | tf_op jit(solution)/shard_map/solve/pallas_call | solution.py:610
  77.3 2.4 %hand_over.1 = (f32[8,8,32,256]{3,2,1,0:T(8,128)}, f32[8,16]{1,0:T(8,128)}) custom-call(f32[8,8,32,256]{3,2,1,0:T(8,128)} %get-tuple-element.4.solved_ref, f32[8,16]{1,0:T(8,128)} %get-tuple-element.5.summed_ref), custom_call_target="tpu_custom_call" | custom-call | tf_op jit(solution)/shard_map/hand_over/pallas_call | solution.py:656
